TPU v7x, 32 devices: a whole 2x2x4 slice. The times are simulated.
32 devices in a mesh: groups: 2 (over y), seq: 4 (over z), head: 2 (over x), layer: 2 (over core).
Axes of the slice: x: 2, y: 2, z: 4, core: 2. Of those that a mesh axis runs over, the one named last changes fastest.
Arguments:
- kv_cache: bfloat16 [2, 2, 8, 4096, 2, 128], P(None, 'layer', 'groups', 'seq', 'head'), parts along dimension 2, may hold values from -800 to 800
- valid_blocks: int32 [8], P('groups'), parts along dimension 0, may hold values from 1 to 32, 64 in all
Outputs:
- decode_cache: bfloat16 [2, 2, 8, 4096, 2, 128], P(None, 'layer', ('groups', 'seq'), None, 'head'), parts along dimension 2
- centers: float32 [2, 2, 8, 2, 128], P(None, 'layer', 'groups', 'head'), parts along dimension 2
- scales: float32 [2, 2, 8, 2, 128], P(None, 'layer', 'groups', 'head'), parts along dimension 2
There are 2 independent parts, one for each index of `groups`. A program takes and returns all parts, laid end to end along the dimension named above; each array names one. Nothing has to cross between parts.
Inputs may be any that keep to these rules, and one draw needn't show every extreme that they name: `valid_blocks`: the counts of the 4 users sum to 64, and the largest equals 32.
All inputs are finite; a program needn't handle non-finite values.
Results may differ from a plain program's by a relative error of at most 0.001.
Values may be sent and summed in bfloat16 or wider, within the bound.
A program may use at most 64 MiB of HBM per device.

v0:
```python
import jax
import jax.numpy as jnp
from jax import lax
from jax.sharding import PartitionSpec as P

BLOCK = 128
epsilon = 1e-06


def on_device(kv_cache, valid_blocks):
    kind_count, layer_dev, user_count, per_dev, heads_dev, head_dim = kv_cache.shape
    owners = lax.axis_size("seq")
    quarter = owners // user_count
    part_len = per_dev // quarter
    seq_index = lax.axis_index("seq")
    lengths = valid_blocks * BLOCK
    values = kv_cache.astype(jnp.float32)
    position = seq_index * per_dev + jnp.arange(per_dev, dtype=jnp.int32)
    is_live = position[None, :] < lengths[:, None]
    live_mask = is_live[None, None, :, :, None, None]
    local_sum = jnp.sum(jnp.where(live_mask, values, 0.0), axis=3)
    user_lengths = lengths.astype(jnp.float32)[None, None, :, None, None]
    totals = lax.psum(local_sum, "seq")
    centers = totals / user_lengths
    local_spread = jnp.max(
        jnp.where(live_mask, jnp.abs(values - centers[:, :, :, None]), 0.0), axis=3
    )
    spread = lax.pmax(local_spread, "seq")
    scales = spread + epsilon
    normed = jnp.where(
        live_mask, (values - centers[:, :, :, None]) / scales[:, :, :, None], 0.0
    ).astype(jnp.bfloat16)
    outgoing = normed.reshape(
        kind_count, layer_dev, user_count * quarter, part_len, heads_dev, head_dim
    )
    received = lax.all_to_all(outgoing, "seq", split_axis=2, concat_axis=2, tiled=True)
    arranged = received.reshape(kind_count, layer_dev, 1, owners * part_len, heads_dev, head_dim)
    return (arranged, centers, scales)


def solution(mesh):
    in_specs = (P(None, "layer", "groups", "seq", "head", None), P("groups"))
    out_specs = (
        P(None, "layer", ("groups", "seq"), None, "head", None),
        P(None, "layer", "groups", "head", None),
        P(None, "layer", "groups", "head", None),
    )
    return jax.shard_map(
        on_device, mesh=mesh, in_specs=in_specs, out_specs=out_specs, check_vma=False
    )
```

profile of v0, /device:TPU:0, one launch (start us, length us, event | category | flops | bytes accessed | tf_op | source)
XLA Modules:
  0.0 79.4 jit_solution(9776314781821777403)
XLA Ops:
  0.6 0.0 copy-start
  0.6 0.8 %fusion.7 = (f32[4]{0:T(128)S(1)}, s32[4]{0:T(128)S(1)}) fusion(s32[4]{0:T(128)} %param.3), kind=kLoop, calls=%fused_computation.14 | loop fusion | flops 8 | bytes 48 | tf_op jit(solution)/shard_map/convert_element_type | solution.py:22
  1.5 0.1 broadcast_compare_fusion
  1.5 2.8 %fusion.6 = f32[2,4,128]{2,0,1:T(2,128)S(1)} fusion(pred[4,1024]{1,0:T(4,128)(4,1)S(1)} %broadcast_compare_fusion, bf16[2,1,4,1024,1,128]{5,3,4,2,1,0:T(8,128)(2,1)} %param.2), kind=kLoop, calls=%fused_computation.8 | loop fusion | flops 3144704 | bytes 2105344 | tf_op jit(solution)/shard_map/reduce_sum | solution.py:21
  4.3 13.5 %psum.7 = f32[2,1,4,1,128]{4,0,2,3,1:T(2,128)S(1)} all-reduce(f32[2,1,4,1,128]{4,0,2,3,1:T(2,128)S(1)} %bitcast.10), channel_id=1, replica_groups=mesh['groups'=2,'seq'=4,'head'=2,'layer'=2] {'seq'}, use_global_device_ids=true, to_apply=%region_1.2 | all-reduce | flops 1024 | bytes 8192 | tf_op jit(solution)/shard_map/psum | solution.py:23
  17.8 0.1 fusion.9
  17.9 0.0 copy-done
  17.9 1.0 %fusion.3 = f32[2,4,128]{2,0,1:T(2,128)S(1)} fusion(f32[2,4,128]{2,0,1:T(2,128)S(1)} %fusion.9, pred[4,1024]{1,0:T(4,128)(4,1)S(1)} %broadcast_compare_fusion, bf16[2,1,4,1024,1,128]{5,3,4,2,1,0:T(8,128)(2,1)S(1)} %copy-done), kind=kLoop, calls=%fused_computation.5 | loop fusion | flops 5241856 | bytes 2109440 | tf_op jit(solution)/shard_map/reduce_max | solution.py:25
  18.9 8.4 %pmax.7 = f32[2,1,4,1,128]{4,0,2,3,1:T(2,128)S(1)} all-reduce(f32[2,1,4,1,128]{4,0,2,3,1:T(2,128)S(1)} %bitcast.11), channel_id=1, replica_groups=mesh['groups'=2,'seq'=4,'head'=2,'layer'=2] {'seq'}, use_global_device_ids=true, to_apply=%region_3.4 | all-reduce | flops 1024 | bytes 8192 | tf_op jit(solution)/shard_map/pmax | solution.py:28
  27.3 2.4 %fusion.5 = bf16[2,1,4,1024,1,128]{5,3,4,1,0,2:T(8,128)(2,1)} fusion(f32[2,4,128]{2,0,1:T(2,128)S(1)} %get-tuple-element.10, f32[2,4,128]{2,0,1:T(2,128)S(1)} %fusion.9, pred[4,1024]{1,0:T(4,128)(4,1)S(1)} %broadcast_compare_fusion, bf16[2,1,4,1024,1,128]{5,3,4,2,1,0:T(8,128)(2,1)S(1)} %copy-done), kind=kLoop, calls=%fused_computation.7 | loop fusion | flops 5242880 | bytes 4206592 | tf_op jit(solution)/shard_map/convert_element_type | solution.py:32
  29.7 3.6 %all-to-all-start = ((bf16[2,1,4,1024,1,128]{5,3,4,1,0,2:T(8,128)(2,1)}), bf16[2,1,4,1024,1,128]{5,3,4,1,0,2:T(8,128)(2,1)S(1)}, u32[]{:S(2)}, u32[]{:S(2)}) async-start(bf16[2,1,4,1024,1,128]{5,3,4,1,0,2:T(8,128)(2,1)} %fusion.5), calls=%async_computation | async-start | bytes 4194304 | tf_op jit(solution)/shard_map/all_to_all | solution.py:36
  33.3 0.1 broadcast_divide_fusion
  33.4 0.6 copy.16
  34.0 0.6 copy.17
  34.6 43.4 %all-to-all-done = bf16[2,1,4,1024,1,128]{5,3,4,1,0,2:T(8,128)(2,1)S(1)} async-done(((bf16[2,1,4,1024,1,128]{5,3,4,1,0,2:T(8,128)(2,1)}), bf16[2,1,4,1024,1,128]{5,3,4,1,0,2:T(8,128)(2,1)S(1)}, u32[]{:S(2)}, u32[]{:S(2)}) %all-to-all-start) | async-done | bytes 2097184 | tf_op jit(solution)/shard_map/all_to_all | solution.py:36
  77.9 1.5 %copy.14 = bf16[2,1,4,1024,1,128]{5,3,2,0,4,1:T(8,128)(2,1)} copy(bf16[2,1,4,1024,1,128]{5,3,4,1,0,2:T(8,128)(2,1)S(1)} %all-to-all-done) | data formatting | bytes 4194304 | tf_op jit(solution)/shard_map/all_to_all | solution.py:36
  (2 shorter events, 0.0 us)
Async XLA Ops:
  0.6 17.2 %copy-start = (bf16[2,1,4,1024,1,128]{5,3,4,2,1,0:T(8,128)(2,1)S(1)}, bf16[2,1,4,1024,1,128]{5,3,4,2,1,0:T(8,128)(2,1)}, u32[]{:S(2)}) copy-start(bf16[2,1,4,1024,1,128]{5,3,4,2,1,0:T(8,128)(2,1)} %param.2) | copy-start | bytes 6291460
  29.7 48.3 %all-to-all-start = ((bf16[2,1,4,1024,1,128]{5,3,4,1,0,2:T(8,128)(2,1)}), bf16[2,1,4,1024,1,128]{5,3,4,1,0,2:T(8,128)(2,1)S(1)}, u32[]{:S(2)}, u32[]{:S(2)}) async-start(bf16[2,1,4,1024,1,128]{5,3,4,1,0,2:T(8,128)(2,1)} %fusion.5), calls=%async_computation | async-start | bytes 4194304 | tf_op jit(solution)/shard_map/all_to_all | solution.py:36
where the time goes:
time: 79.7 us; the launch traced here: 79.4 us
  waiting for transfers between devices  43.4 us (54%)
  blocking collectives  21.9 us (27%)
  other arithmetic  7.21 us (9%)
  starting transfers between devices  3.61 us (5%)
  local copies, waits for them, and re-layouts  2.66 us (3%)
    all_to_all x1, waiting for transfers between devices, on_device(): lax.all_to_all(outgoing, 'seq', split_axis=2, concat_axis=2, tiled=True)  43.4 us
    psum x1, blocking collectives, on_device(): totals = lax.psum(local_sum, 'seq')  13.5 us
    pmax x1, blocking collectives, on_device(): spread = lax.pmax(local_spread, 'seq')  8.38 us
    all_to_all x1, starting transfers between devices, on_device(): lax.all_to_all(outgoing, 'seq', split_axis=2, concat_axis=2, tiled=True)  3.61 us
    reduce_sum x1, other arithmetic, on_device(): local_sum = jnp.sum(jnp.where(live_mask, values, 0.0), axis=3)  2.76 us
    convert_element_type x1, other arithmetic, on_device(): normed = jnp.where(live_mask, (values - centers[:, :, :, None]) / scales[...  2.37 us
  transfers between devices with their start and end apart: 1, of which 1 were waited for; matrix products, arithmetic and copies ran while one was open for 2% of the time, Pallas kernels for 0%

commit v1 on v0

--- a/solution.py
+++ b/solution.py
@@ -33,7 +33,10 @@
     outgoing = normed.reshape(
         kind_count, layer_dev, user_count * quarter, part_len, heads_dev, head_dim
     )
-    received = lax.all_to_all(outgoing, "seq", split_axis=2, concat_axis=2, tiled=True)
+    received = jnp.concatenate(
+        lax.all_to_all(jnp.stack(jnp.split(outgoing, lax.axis_size("seq"), axis=2)), "seq", 0, 0),
+        axis=2,
+    )
     arranged = received.reshape(kind_count, layer_dev, 1, owners * part_len, heads_dev, head_dim)
     return (arranged, centers, scales)
 

time: 79.7 us -> 77.2 us (0.969)
  blocking collectives: 21.9 us -> 69.4 us
  waiting for transfers between devices: 43.4 us -> 0 us
  starting transfers between devices: 3.61 us -> 0 us
  other arithmetic: 7.21 us -> 5.24 us
  local copies, waits for them, and re-layouts: 2.66 us -> 1.61 us
    all_to_all x0 -> x1, blocking collectives: none -> 47.5 us  [on_device(): lax.all_to_all(jnp.stack(jnp.split(outgoing, lax.axis_size('seq'), axis=2...]
    all_to_all x1 -> x0, waiting for transfers between devices: 43.4 us -> none  [on_device(): lax.all_to_all(outgoing, 'seq', split_axis=2, concat_axis=2, tiled=True)]
    all_to_all x1 -> x0, starting transfers between devices: 3.61 us -> none  [on_device(): lax.all_to_all(outgoing, 'seq', split_axis=2, concat_axis=2, tiled=True)]
    all_to_all x1 -> x0, local copies, waits for them, and re-layouts: 1.45 us -> none  [on_device(): lax.all_to_all(outgoing, 'seq', split_axis=2, concat_axis=2, tiled=True)]
    reshape x0 -> x1, local copies, waits for them, and re-layouts: none -> 1.45 us  [on_device(): jnp.concatenate(lax.all_to_all(jnp.stack(jnp.split(outgoing, lax.axis_siz...]
    convert_element_type x1, other arithmetic: 2.37 us -> 1.02 us  [on_device(): normed = jnp.where(live_mask, (values - centers[:, :, :, None]) / scales[...]
    unnamed x4 -> x6, local copies, waits for them, and re-layouts: 1.21 us -> 0.01 us
    reduce_sum x1, other arithmetic: 2.76 us -> 1.95 us  [on_device(): local_sum = jnp.sum(jnp.where(live_mask, values, 0.0), axis=3)]
  transfers between devices with their start and end apart: 1 -> 0, of which waited for: 1 -> 0; matrix products, arithmetic and copies ran while one was open for 2% -> 0% of each run, Pallas kernels for 0% -> 0%
where the time goes in v1:
time: 77.2 us; the launch traced here: 77 us
  blocking collectives  69.4 us (90%)
  other arithmetic  5.24 us (7%)
  local copies, waits for them, and re-layouts  1.61 us (2%)
    all_to_all x1, blocking collectives, on_device(): lax.all_to_all(jnp.stack(jnp.split(outgoing, lax.axis_size('seq'), axis=2...  47.5 us
    psum x1, blocking collectives, on_device(): totals = lax.psum(local_sum, 'seq')  13.5 us
    pmax x1, blocking collectives, on_device(): spread = lax.pmax(local_spread, 'seq')  8.38 us
    reduce_sum x1, other arithmetic, on_device(): local_sum = jnp.sum(jnp.where(live_mask, values, 0.0), axis=3)  1.95 us

profile of v1, /device:TPU:0, one launch (start us, length us, event | category | flops | bytes accessed | tf_op | source)
XLA Modules:
  0.0 77.0 jit_solution(12210359469958879802)
XLA Ops:
  0.6 0.0 copy-start
  0.6 0.8 %fusion.7 = (f32[4]{0:T(128)S(1)}, s32[4]{0:T(128)S(1)}) fusion(s32[4]{0:T(128)} %param.3), kind=kLoop, calls=%fused_computation.19 | loop fusion | flops 8 | bytes 48 | tf_op jit(solution)/shard_map/convert_element_type | solution.py:22
  1.5 0.1 broadcast_compare_fusion
  1.5 1.9 %fusion.6 = f32[2,4,128]{2,1,0:T(4,128)S(1)} fusion(bf16[2,1,4,1024,1,128]{5,3,4,2,1,0:T(8,128)(2,1)} %param.2, pred[4,1024]{1,0:T(4,128)(4,1)S(1)} %broadcast_compare_fusion), kind=kLoop, calls=%fused_computation.8 | loop fusion | flops 3144704 | bytes 2105344 | tf_op jit(solution)/shard_map/reduce_sum | solution.py:21
  3.5 13.5 %psum.7 = f32[2,1,4,1,128]{4,3,2,1,0:T(1,128)S(1)} all-reduce(f32[2,1,4,1,128]{4,3,2,1,0:T(1,128)S(1)} %bitcast.25), channel_id=1, replica_groups=mesh['groups'=2,'seq'=4,'head'=2,'layer'=2] {'seq'}, use_global_device_ids=true, to_apply=%region_1.2 | all-reduce | flops 1024 | bytes 8192 | tf_op jit(solution)/shard_map/psum | solution.py:23
  17.0 0.1 broadcast_divide_fusion
  17.1 0.0 copy-start.1
  17.1 0.0 copy-done
  17.1 1.0 %fusion.3 = f32[2,4,128]{2,1,0:T(4,128)S(1)} fusion(bf16[2,1,4,1024,1,128]{5,3,4,2,1,0:T(8,128)(2,1)S(1)} %copy-done, f32[2,4,128]{2,1,0:T(4,128)S(1)} %bitcast.22, pred[4,1024]{1,0:T(4,128)(4,1)S(1)} %broadcast_compare_fusion), kind=kLoop, calls=%fused_computation.5 | loop fusion | flops 5241856 | bytes 2109440 | tf_op jit(solution)/shard_map/reduce_max | solution.py:25
  18.1 8.4 %pmax.7 = f32[2,1,4,1,128]{4,3,2,1,0:T(1,128)S(1)} all-reduce(f32[2,1,4,1,128]{4,3,2,1,0:T(1,128)S(1)} %bitcast.26), channel_id=1, replica_groups=mesh['groups'=2,'seq'=4,'head'=2,'layer'=2] {'seq'}, use_global_device_ids=true, to_apply=%region_3.4 | all-reduce | flops 1024 | bytes 8192 | tf_op jit(solution)/shard_map/pmax | solution.py:28
  26.5 0.0 copy-start.2
  26.5 1.0 %fusion.5 = bf16[2,1,4,1024,1,128]{5,3,4,2,1,0:T(8,128)(2,1)S(1)} fusion(bf16[2,1,4,1024,1,128]{5,3,4,2,1,0:T(8,128)(2,1)S(1)} %copy-done, f32[2,4,128]{2,1,0:T(4,128)S(1)} %bitcast.24, f32[2,4,128]{2,1,0:T(4,128)S(1)} %bitcast.23, pred[4,1024]{1,0:T(4,128)(4,1)S(1)} %broadcast_compare_fusion), kind=kLoop, calls=%fused_computation.7 | loop fusion | flops 5242880 | bytes 4206592 | tf_op jit(solution)/shard_map/convert_element_type | solution.py:32
  27.5 0.0 copy-done.1
  27.5 0.0 copy-done.2
  27.6 0.1 slice_bitcast_fusion.3
  27.7 0.3 pad_maximum_fusion
  28.0 47.5 %all_to_all.5 = bf16[4,2,1,1,1024,1,128]{6,4,1,5,3,2,0:T(8,128)(2,1)S(1)} all-to-all(bf16[4,2,1,1,1024,1,128]{6,4,1,5,3,2,0:T(8,128)(2,1)S(1)} %pad_maximum_fusion), channel_id=1, replica_groups=mesh['groups'=2,'seq'=4,'head'=2,'layer'=2] {'seq'}, dimensions={0} | all-to-all | bytes 4194304 | tf_op jit(solution)/shard_map/all_to_all | solution.py:37
  75.5 1.5 %copy.8 = bf16[2,1,4,1,1024,1,128]{6,4,2,0,5,3,1:T(8,128)(2,1)} copy(bf16[2,1,4,1,1024,1,128]{6,4,0,5,3,1,2:T(8,128)(2,1)S(1)} %bitcast.20) | data formatting | bytes 4194304 | tf_op jit(solution)/shard_map/reshape | solution.py:36
  (2 shorter events, 0.0 us)
Async XLA Ops:
  0.6 16.4 %copy-start = (bf16[2,1,4,1024,1,128]{5,3,4,2,1,0:T(8,128)(2,1)S(1)}, bf16[2,1,4,1024,1,128]{5,3,4,2,1,0:T(8,128)(2,1)}, u32[]{:S(2)}) copy-start(bf16[2,1,4,1024,1,128]{5,3,4,2,1,0:T(8,128)(2,1)} %param.2) | copy-start | bytes 6291460
  17.1 10.5 %copy-start.1 = (f32[2,1,4,1,128]{4,3,2,1,0:T(1,128)}, f32[2,1,4,1,128]{4,3,2,1,0:T(1,128)S(1)}, u32[]{:S(2)}) copy-start(f32[2,1,4,1,128]{4,3,2,1,0:T(1,128)S(1)} %broadcast_divide_fusion) | copy-start | bytes 12292
  26.5 1.0 %copy-start.2 = (f32[2,1,4,1,128]{4,3,2,1,0:T(1,128)}, f32[2,1,4,1,128]{4,3,2,1,0:T(1,128)S(1)}, u32[]{:S(2)}) copy-start(f32[2,1,4,1,128]{4,3,2,1,0:T(1,128)S(1)} %broadcast_add_fusion) | copy-start | bytes 12292
